TPU v7x, 32 devices: a whole 2x2x4 slice. The times are simulated.
32 devices in a mesh: grp: 2 (over x), wide: 16 (over z, y, core).
Axes of the slice: x: 2, y: 2, z: 4, core: 2. Of those that a mesh axis runs over, the one named last changes fastest.
Arguments:
- x_pool: bfloat16 [16384, 7168], P(('grp', 'wide')), may hold values from -6 to 6
- token_ids: int32 [4096], P(('grp', 'wide')), may hold values from 0 to 16383, as said below
- cotangent: bfloat16 [4096, 7168], P(('grp', 'wide')), may hold values from -6 to 6
- gate_up: bfloat16 [2, 1024, 7168], P(None, 'wide', 'grp'), may hold values from -0.0625 to 0.0625
- down_weight: bfloat16 [1024, 7168], P('wide', 'grp'), may hold values from -0.1875 to 0.1875
- loss_exponent: int32 [1], replicated, may hold values from 3 to 9
Outputs:
- grad_gate_up: bfloat16 [2, 1024, 7168], P(None, 'wide', 'grp')
- grad_down: bfloat16 [1024, 7168], P('wide', 'grp')
Inputs may be any that keep to these rules, and one draw needn't show every extreme that they name: The 128 ids in aligned block b of token_ids name rows b * 512 to (b + 1) * 512 - 1 of x_pool.
All inputs are finite; a program needn't handle non-finite values.
Results may differ from a plain program's by a relative error of at most 0.014.
Values may be sent and summed in bfloat16 or wider, within the bound.
No kernel may reach another device: no remote copies, remote signals or barrier semaphores. Data moves between devices by JAX's collectives and lax.ppermute only.
A program may use at most 192 MiB of HBM per device.

v0:
```python
import jax
import jax.numpy as jnp
import numpy as np
from jax import lax
from jax.sharding import PartitionSpec as P

BLOCKS = 8


def swapped(value, axis, bit):
    mask = 2**bit
    pairs = [(source, source ^ mask) for source in range(lax.axis_size(axis))]
    return lax.ppermute(value, axis, pairs)


def unscale_of(loss_exponent):
    levels = jnp.arange(16, dtype=jnp.int32)
    powers = jnp.asarray(np.power(0.5, np.arange(16)), dtype=jnp.float32)
    return jnp.sum(jnp.where(levels == loss_exponent[0], powers, jnp.float32(0.0)))


def contract_last(left_side, right_side):
    return lax.dot_general(
        left_side, right_side, (((1,), (1,)), ((), ())), preferred_element_type=jnp.float32
    )


def contract_first(left_side, right_side):
    return lax.dot_general(
        left_side, right_side, (((0,), (0,)), ((), ())), preferred_element_type=jnp.float32
    )


def halve_blocks(gradients, wide_index, low_bits):
    for bit_index in reversed(range(low_bits)):
        half_units = gradients.shape[1] // 2
        lower_half = gradients[:, :half_units]
        upper_half = gradients[:, half_units:]
        own_bit = wide_index >> bit_index & 1
        kept_half = jnp.where(own_bit == 0, lower_half, upper_half)
        sent_half = jnp.where(own_bit == 0, upper_half, lower_half).astype(jnp.bfloat16)
        arrived = swapped(sent_half, "wide", bit_index)
        gradients = kept_half + arrived.astype(jnp.float32)
    return gradients


def per_device(x_pool, token_ids, cotangent, gate_up, down_weight, loss_exponent):
    wide_count = lax.axis_size("wide")
    group_count = wide_count // BLOCKS
    low_bits = group_count.bit_length() - 1
    wide_index = lax.axis_index("wide")
    device_index = lax.axis_index("grp") * wide_count + wide_index
    local_rows = token_ids - device_index * x_pool.shape[0]
    picked = jnp.take(x_pool, local_rows, axis=0)
    stacked = jnp.stack([picked, cotangent])
    token_count = stacked.shape[1]
    model_width = stacked.shape[2]
    weight_tile = jnp.concatenate([gate_up, down_weight[None]], axis=0)
    weight_rows = lax.all_gather(weight_tile, "grp", axis=2, tiled=True)
    for bit_index in range(low_bits):
        partner = swapped(weight_rows, "wide", bit_index)
        own_bit = wide_index >> bit_index & 1
        weight_rows = jnp.where(
            own_bit == 0,
            jnp.concatenate([weight_rows, partner], axis=1),
            jnp.concatenate([partner, weight_rows], axis=1),
        )
    hidden_units = weight_rows.shape[1]
    slot_rows = token_count // group_count
    quarters = stacked.reshape(2, group_count, slot_rows, model_width)
    outgoing = jnp.broadcast_to(quarters[:, None], (2, BLOCKS, group_count, slot_rows, model_width))
    outgoing = outgoing.reshape(2, wide_count * slot_rows, model_width)
    gathered = lax.all_to_all(outgoing, "wide", split_axis=1, concat_axis=1, tiled=True)
    tokens_in = gathered[0]
    tokens_grad = gathered[1]
    unscale = unscale_of(loss_exponent)
    gate_up_rows = weight_rows[:2].reshape(2 * hidden_units, model_width)
    projected = contract_last(tokens_in, gate_up_rows)
    gate_act = projected[:, :hidden_units]
    up_act = projected[:, hidden_units:]
    delta_hidden = unscale * contract_last(tokens_grad, weight_rows[2])
    sigmoid_gate = jax.nn.sigmoid(gate_act)
    hidden = (gate_act * sigmoid_gate * up_act).astype(jnp.bfloat16)
    delta_gate = (
        delta_hidden * up_act * sigmoid_gate * (1.0 + gate_act * (1.0 - sigmoid_gate))
    ).astype(jnp.bfloat16)
    delta_up = (delta_hidden * gate_act * sigmoid_gate).astype(jnp.bfloat16)
    delta_pair = jnp.concatenate([delta_gate, delta_up], axis=1)
    grad_pair = contract_first(delta_pair, tokens_in)
    grad_hidden = unscale * contract_first(hidden, tokens_grad)
    gradients = jnp.concatenate([grad_pair, grad_hidden], axis=0).reshape(
        3, hidden_units, model_width
    )
    gradients = halve_blocks(gradients, wide_index, low_bits)
    gradients = lax.psum_scatter(
        gradients.astype(jnp.bfloat16), "grp", scatter_dimension=2, tiled=True
    ).astype(jnp.float32)
    finished = gradients.astype(jnp.bfloat16)
    return (finished[:2], finished[2])


def solution(mesh):
    in_specs = (
        P(("grp", "wide"), None),
        P(("grp", "wide")),
        P(("grp", "wide"), None),
        P(None, "wide", "grp"),
        P("wide", "grp"),
        P(),
    )
    out_specs = (P(None, "wide", "grp"), P("wide", "grp"))
    return jax.shard_map(
        per_device, mesh=mesh, in_specs=in_specs, out_specs=out_specs, check_vma=False
    )
```

profile of v0, /device:TPU:0, one launch (start us, length us, event | category | flops | bytes accessed | tf_op | source)
XLA Modules:
  0.0 880.1 jit_solution(12923270134924933211)
XLA Ops:
  7.9 7.4 gather_fusion
  15.6 1.8 maximum_bitcast_fusion
  17.4 3.8 copy.10
  21.2 17.6 %broadcast_in_dim.34 = bf16[2,8,2,64,7168]{4,0,3,2,1:T(2,128)(2,1)} broadcast(bf16[2,2,64,7168]{3,0,2,1:T(2,128)(2,1)S(1)} %copy.10), dimensions={0,2,3,4} | broadcast | bytes 33030144 | tf_op jit(solution)/shard_map/broadcast_in_dim | solution.py:71
  38.8 7.6 all-to-all-start
  46.5 1.2 pad_maximum_fusion.1
  48.0 42.6 %all-gather.2.cloned.1.call-done = bf16[3,64,7168]{2,1,0:T(8,128)(2,1)} async-done(((bf16[3,64,3584]{2,1,0:T(8,128)(2,1)}), bf16[3,64,7168]{2,1,0:T(8,128)(2,1)}) %all-gather.2.cloned.1.call-update) | async-done | bytes 2752528 | tf_op jit(solution)/shard_map/all_gather | solution.py:59
  91.8 4.0 collective-permute-done
  95.9 4.3 maximum_select_fusion
  100.2 2.4 copy-done
  102.6 2.2 slice.45
  104.8 457.4 %all-to-all-done = bf16[2,1024,7168]{2,0,1:T(2,128)(2,1)} async-done(((bf16[2,1024,7168]{2,0,1:T(2,128)(2,1)}), bf16[2,1024,7168]{2,0,1:T(2,128)(2,1)}, u32[]{:S(2)}, u32[]{:S(2)}) %all-to-all-start) | async-done | bytes 29360160 | tf_op jit(solution)/shard_map/all_to_all | solution.py:73
  562.2 55.9 %fusion.11 = (bf16[1,1024,7168]{2,0,1:T(2,128)(2,1)}, bf16[1,1024,7168]{2,0,1:T(2,128)(2,1)}) fusion(bf16[2,1024,7168]{2,0,1:T(2,128)(2,1)} %all-to-all-done), kind=kLoop, calls=%fused_computation.32 | loop fusion | bytes 58720256 | tf_op jit(solution)/shard_map/slice | solution.py:74
  618.1 18.2 %fusion.2 = f32[1024,256]{0,1:T(8,128)S(1)} fusion(bf16[256,7168]{1,0:T(8,128)(2,1)S(1)} %bitcast.36, bf16[1,1024,7168]{2,0,1:T(2,128)(2,1)} %get-tuple-element.4), kind=kOutput, calls=%fused_computation.7 | convolution fusion | flops 3758096384 | bytes 19398656 | tf_op jit(solution)/shard_map/dot_general | solution.py:23
  636.3 16.1 %multiply_convert_fusion.2 = (bf16[1024,128]{0,1:T(8,128)(2,1)S(1)}, bf16[1024,128]{0,1:T(8,128)(2,1)S(1)}) fusion(f32[1024,256]{0,1:T(8,128)S(1)} %fusion.2, bf16[3,128,7168]{2,1,0:T(8,128)(2,1)} %copy-done, bf16[1,1024,7168]{2,0,1:T(2,128)(2,1)} %get-tuple-element.5, f32[]{:T(128)} %fusion.8), kind=kOutput, calls=%fused_computation.21 | convolution fusion | flops 1880883200 | bytes 32768512 | tf_op jit(solution)/shard_map/dot_general | solution.py:23
  652.4 17.1 %convolution_multiply_fusion = f32[128,7168]{1,0:T(8,128)} fusion(bf16[1,1024,7168]{2,0,1:T(2,128)(2,1)} %get-tuple-element.5, f32[]{:T(128)} %fusion.8, f32[1024,256]{0,1:T(8,128)S(1)} %fusion.2), kind=kOutput, calls=%fused_computation.4 | convolution fusion | flops 1880752128 | bytes 19398660 | tf_op jit(solution)/shard_map/dot_general | solution.py:29
  669.6 17.7 %fusion.1 = f32[256,7168]{1,0:T(8,128)} fusion(bf16[1,1024,7168]{2,0,1:T(2,128)(2,1)} %get-tuple-element.4, bf16[1024,128]{0,1:T(8,128)(2,1)S(1)} %get-tuple-element.7, bf16[1024,128]{0,1:T(8,128)(2,1)S(1)} %get-tuple-element.6), kind=kOutput, calls=%fused_computation.6 | convolution fusion | flops 3759144960 | bytes 22544384 | tf_op jit(solution)/shard_map/dot_general | solution.py:29
  687.3 9.6 %pad_maximum_fusion = f32[384,7168]{1,0:T(8,128)} fusion(f32[128,7168]{1,0:T(8,128)} %convolution_multiply_fusion, f32[256,7168]{1,0:T(8,128)} %fusion.1), kind=kLoop, calls=%fused_computation.3 | loop fusion | flops 2752512 | bytes 22020096 | tf_op jit(solution)/shard_map/concatenate | solution.py:91
  696.9 4.7 select_convert_fusion
  702.6 4.7 collective-permute-done.1
  707.3 7.1 add_convert_fusion
  714.5 154.8 %reduce-scatter.2.cloned.1.call-done = bf16[3,64,3584]{2,1,0:T(8,128)(2,1)} async-done(((bf16[3,64,7168]{2,1,0:T(8,128)(2,1)}), bf16[3,64,3584]{2,1,0:T(8,128)(2,1)}) %reduce-scatter.2.cloned.1.call-update) | async-done | bytes 1376272 | tf_op jit(solution)/shard_map/reduce_scatter | solution.py:95
  869.3 2.2 slice.50
  871.4 1.8 slice_bitcast_fusion.4
  (20 shorter events, 2.9 us)
Async XLA Ops:
  38.8 7.7 copy-start.2
  38.8 7.7 copy-start.3
  38.8 52.4 %copy-start.4 = (f32[16]{0:T(128)S(1)}, f32[16]{0:T(128)}, u32[]{:S(2)}) copy-start(f32[16]{0:T(128)} %constant.37.clone) | copy-start | bytes 196
  38.8 523.3 %all-to-all-start = ((bf16[2,1024,7168]{2,0,1:T(2,128)(2,1)}), bf16[2,1024,7168]{2,0,1:T(2,128)(2,1)}, u32[]{:S(2)}, u32[]{:S(2)}) async-start(bf16[2,1024,7168]{2,0,1:T(2,128)(2,1)} %bitcast.32), calls=%async_computation | async-start | bytes 58720256 | tf_op jit(solution)/shard_map/all_to_all | solution.py:73
  46.4 44.1 %all-gather.2.cloned.1.call-start = ((), (), s32[]{:S(2)}) async-start(), calls=%async_computation.2 | async-start | bytes 4128768 | tf_op jit(solution)/shard_map/all_gather | solution.py:59
  47.7 821.5 %reduce-scatter.2.cloned.1.call-start = ((), (), s32[]{:S(2)}) async-start(), calls=%async_computation.3 | async-start | bytes 4128768 | tf_op jit(solution)/shard_map/reduce_scatter | solution.py:95
  90.6 5.3 collective-permute-start
  100.2 2.4 copy-start
  562.2 55.9 %copy-start.1 = (bf16[2,128,7168]{2,1,0:T(8,128)(2,1)S(1)}, bf16[2,128,7168]{2,1,0:T(8,128)(2,1)}, u32[]{:S(2)}) copy-start(bf16[2,128,7168]{2,1,0:T(8,128)(2,1)} %slice.45) | copy-start | bytes 11010052
  701.6 5.8 collective-permute-start.1
Sparse Core Ops, SparseCore 0:
  48.8 41.7 all-gather.1
  714.6 154.6 reduce-scatter.1
where the time goes:
time: 881 us; the launch traced here: 880 us
  waiting for transfers between devices  664 us (75%)
  local copies, waits for them, and re-layouts  93.3 us (11%)
  matrix products  69.2 us (8%)
  other arithmetic  30.3 us (3%)
  between operations  14.8 us (2%)
  starting transfers between devices  8.9 us (1%)
    all_to_all x1, waiting for transfers between devices, per_device(): lax.all_to_all(outgoing, 'wide', split_axis=1, concat_axis=1, tiled=True)  457 us
    reduce_scatter x1, waiting for transfers between devices, per_device(): lax.psum_scatter(gradients.astype(jnp.bfloat16), 'grp', scatter_dimension...  155 us
    slice x1, local copies, waits for them, and re-layouts, per_device(): tokens_in = gathered[0]  55.9 us
    all_gather x1, waiting for transfers between devices, per_device(): weight_rows = lax.all_gather(weight_tile, 'grp', axis=2, tiled=True)  42.6 us
    dot_general x2, matrix products, contract_first(): lax.dot_general(left_side, right_side, (((0,), (0,)), ((), ())), preferre...  34.8 us
    dot_general x2, matrix products, contract_last(): lax.dot_general(left_side, right_side, (((1,), (1,)), ((), ())), preferre...  34.3 us
    broadcast_in_dim x2, local copies, waits for them, and re-layouts, per_device(): jnp.broadcast_to(quarters[:, None], (2, BLOCKS, group_count, slot_rows, m...  21.4 us
  transfers between devices with their start and end apart: 5, of which 5 were waited for; matrix products, arithmetic and copies ran while one was open for 1% of the time, Pallas kernels for 0%

commit v1 on v0

--- a/solution.py
+++ b/solution.py
@@ -70,7 +70,10 @@
     quarters = stacked.reshape(2, group_count, slot_rows, model_width)
     outgoing = jnp.broadcast_to(quarters[:, None], (2, BLOCKS, group_count, slot_rows, model_width))
     outgoing = outgoing.reshape(2, wide_count * slot_rows, model_width)
-    gathered = lax.all_to_all(outgoing, "wide", split_axis=1, concat_axis=1, tiled=True)
+    gathered = jnp.concatenate(
+        lax.all_to_all(jnp.stack(jnp.split(outgoing, lax.axis_size("wide"), axis=1)), "wide", 0, 0),
+        axis=1,
+    )
     tokens_in = gathered[0]
     tokens_grad = gathered[1]
     unscale = unscale_of(loss_exponent)

time: 881 us -> 818 us (0.928)
  matrix products: 69.2 us -> 26 us
  local copies, waits for them, and re-layouts: 93.3 us -> 73.9 us
    slice x1, local copies, waits for them, and re-layouts: 55.9 us -> 11.6 us  [per_device(): tokens_in = gathered[0]]
    unnamed x10 -> x25, local copies, waits for them, and re-layouts: 2.41 us -> 37.4 us
    dot_general x2, matrix products: 34.8 us -> 11.9 us  [contract_first(): lax.dot_general(left_side, right_side, (((0,), (0,)), ((), ())), preferre...]
    dot_general x2, matrix products: 34.3 us -> 14.1 us  [contract_last(): lax.dot_general(left_side, right_side, (((1,), (1,)), ((), ())), preferre...]
    broadcast_in_dim x2 -> x1, local copies, waits for them, and re-layouts: 21.4 us -> 9.98 us  [per_device(): jnp.broadcast_to(quarters[:, None], (2, BLOCKS, group_count, slot_rows, m...]
where the time goes in v1:
time: 818 us
  waiting for transfers between devices  664 us (81%)
  local copies, waits for them, and re-layouts  73.9 us (9%)
  other arithmetic  30.4 us (4%)
  matrix products  26 us (3%)
  between operations  14.8 us (2%)
  starting transfers between devices  8.89 us (1%)
    all_to_all x1, waiting for transfers between devices, per_device(): lax.all_to_all(jnp.stack(jnp.split(outgoing, lax.axis_size('wide'), axis=...  457 us
    reduce_scatter x1, waiting for transfers between devices, per_device(): lax.psum_scatter(gradients.astype(jnp.bfloat16), 'grp', scatter_dimension...  155 us
    all_gather x1, waiting for transfers between devices, per_device(): weight_rows = lax.all_gather(weight_tile, 'grp', axis=2, tiled=True)  42.6 us
    unnamed x25, local copies, waits for them, and re-layouts  37.4 us
  transfers between devices with their start and end apart: 5, of which 5 were waited for; matrix products, arithmetic and copies ran while one was open for 1% of the time, Pallas kernels for 0%

profile of v1, /device:TPU:0, one launch (start us, length us, event | category | flops | bytes accessed | tf_op | source)
XLA Modules:
  0.0 817.5 jit_solution(906632149908805377)
XLA Ops:
  7.9 7.4 gather_fusion
  17.4 10.0 %broadcast_in_dim.34 = bf16[2,8,2,64,7168]{4,3,2,1,0:T(8,128)(2,1)} broadcast(bf16[2,2,64,7168]{3,2,1,0:T(8,128)(2,1)S(1)} %maximum_bitcast_fusion), dimensions={0,2,3,4} | broadcast | bytes 33030144 | tf_op jit(solution)/shard_map/broadcast_in_dim | solution.py:71
  27.4 3.0 fusion.16
  30.4 3.6 fusion.15
  34.1 3.6 fusion.14
  37.6 3.6 fusion.13
  41.2 2.9 fusion.12
  47.0 2.9 fusion.10
  49.9 2.9 fusion.9
  63.7 7.6 all-to-all-start
  72.9 42.6 %all-gather.2.cloned.1.call-done = bf16[3,64,7168]{2,1,0:T(8,128)(2,1)} async-done(((bf16[3,64,3584]{2,1,0:T(8,128)(2,1)}), bf16[3,64,7168]{2,1,0:T(8,128)(2,1)}) %all-gather.2.cloned.1.call-update) | async-done | bytes 2752528 | tf_op jit(solution)/shard_map/all_gather | solution.py:59
  116.8 4.0 collective-permute-done
  120.8 4.3 maximum_select_fusion
  129.6 457.5 %all-to-all-done = bf16[16,2,64,7168]{3,2,1,0:T(8,128)(2,1)} async-done(((bf16[16,2,64,7168]{3,2,1,0:T(8,128)(2,1)}), bf16[16,2,64,7168]{3,2,1,0:T(8,128)(2,1)}, u32[]{:S(2)}, u32[]{:S(2)}) %all-to-all-start) | async-done | bytes 29360160 | tf_op jit(solution)/shard_map/all_to_all | solution.py:74
  587.1 11.6 %fusion.26 = (bf16[1,16,64,7168]{3,2,0,1:T(8,128)(2,1)S(1)}, bf16[1,16,64,7168]{3,2,0,1:T(8,128)(2,1)S(1)}) fusion(bf16[2,16,64,7168]{3,2,0,1:T(8,128)(2,1)} %bitcast.21), kind=kLoop, calls=%fused_computation.61 | loop fusion | bytes 58720256 | tf_op jit(solution)/shard_map/slice | solution.py:77
  598.7 6.0 fusion.27
  604.7 8.1 multiply_convert_fusion.2
  612.8 4.7 convolution_multiply_fusion
  617.5 7.2 fusion.18
  624.7 9.6 %pad_maximum_fusion = f32[384,7168]{1,0:T(8,128)} fusion(f32[128,7168]{1,0:T(8,128)} %convolution_multiply_fusion, f32[256,7168]{1,0:T(8,128)} %fusion.18), kind=kLoop, calls=%fused_computation.1 | loop fusion | flops 2752512 | bytes 22020096 | tf_op jit(solution)/shard_map/concatenate | solution.py:94
  634.3 4.7 select_convert_fusion
  640.0 4.7 collective-permute-done.1
  644.7 7.1 add_convert_fusion
  651.9 154.8 %reduce-scatter.2.cloned.1.call-done = bf16[3,64,3584]{2,1,0:T(8,128)(2,1)} async-done(((bf16[3,64,7168]{2,1,0:T(8,128)(2,1)}), bf16[3,64,3584]{2,1,0:T(8,128)(2,1)}) %reduce-scatter.2.cloned.1.call-update) | async-done | bytes 1376272 | tf_op jit(solution)/shard_map/reduce_scatter | solution.py:98
  (35 shorter events, 28.3 us)
Async XLA Ops:
  27.4 25.4 %copy-start = (bf16[2,8,2,64,7168]{4,3,2,1,0:T(8,128)(2,1)S(1)}, bf16[2,8,2,64,7168]{4,3,2,1,0:T(8,128)(2,1)}, u32[]{:S(2)}) copy-start(bf16[2,8,2,64,7168]{4,3,2,1,0:T(8,128)(2,1)} %broadcast_in_dim.34) | copy-start | bytes 88080384
  63.7 7.7 copy-start.2
  63.7 7.7 copy-start.3
  63.7 52.4 %copy-start.4 = (f32[16]{0:T(128)S(1)}, f32[16]{0:T(128)}, u32[]{:S(2)}) copy-start(f32[16]{0:T(128)} %constant.37.clone) | copy-start | bytes 196
  63.7 523.3 %all-to-all-start = ((bf16[16,2,64,7168]{3,2,1,0:T(8,128)(2,1)}), bf16[16,2,64,7168]{3,2,1,0:T(8,128)(2,1)}, u32[]{:S(2)}, u32[]{:S(2)}) async-start(bf16[16,2,64,7168]{3,2,1,0:T(8,128)(2,1)} %fusion.1), calls=%async_computation | async-start | bytes 58720256 | tf_op jit(solution)/shard_map/all_to_all | solution.py:74
  71.3 44.1 %all-gather.2.cloned.1.call-start = ((), (), s32[]{:S(2)}) async-start(), calls=%async_computation.2 | async-start | bytes 4128768 | tf_op jit(solution)/shard_map/all_gather | solution.py:59
  72.6 734.1 %reduce-scatter.2.cloned.1.call-start = ((), (), s32[]{:S(2)}) async-start(), calls=%async_computation.3 | async-start | bytes 4128768 | tf_op jit(solution)/shard_map/reduce_scatter | solution.py:98
  115.5 5.3 collective-permute-start
  125.1 2.5 copy-start.1
  639.0 5.8 collective-permute-start.1
Sparse Core Ops, SparseCore 0:
  73.7 41.7 all-gather.1
  652.0 154.6 reduce-scatter.1
